TPU v7x, 32 devices: a whole 2x2x4 slice. The times are simulated.
32 devices in a mesh: seq: 8 (over z, y), feat: 4 (over x, core).
Axes of the slice: x: 2, y: 2, z: 4, core: 2. Of those that a mesh axis runs over, the one named last changes fastest.
Arguments:
- hidden_in: bfloat16 [4, 2048, 2048], P(None, 'seq'), may hold values from -6 to 6
- w_query: bfloat16 [2048, 256], replicated, may hold values from -0.125 to 0.125
- w_key: bfloat16 [2048, 256], replicated, may hold values from -0.125 to 0.125
- w_value: bfloat16 [2048, 2048], P(None, 'feat'), may hold values from -0.125 to 0.125
- lengths: int32 [4], replicated, may hold values from 1024 to 2048, as said below
- owners: int32 [4], replicated, may hold values from 0 to 7
Outputs:
- mixed: bfloat16 [4, 2048, 2048], P(None, 'seq', 'feat')
- state_quad: float32 [8, 4, 16, 256, 128], P('seq', None, None, 'feat')
- state_low: float32 [8, 4, 16, 17, 128], P('seq', None, 'feat')
- norm_quad: float32 [8, 4, 16, 256], P('seq', None, None, 'feat')
- norm_low: float32 [8, 4, 16, 17], P('seq', None, 'feat')
Inputs may be any that keep to these rules, and one draw needn't show every extreme that they name: `lengths`: every prompt holds 1024 to 2048 live tokens, and some prompt holds exactly 2048. `owners`: several prompts may share a decoding device.
All inputs are finite; a program needn't handle non-finite values.
Results may differ from a plain program's by a relative error of at most 0.0085.
Values may be sent and summed in bfloat16 or wider, within the bound.
A program may use at most 256 MiB of HBM per device.

v0:
```python
import functools

import jax
import jax.numpy as jnp
from jax import lax
from jax.experimental import pallas as pl
from jax.experimental.pallas import tpu as pltpu
from jax.sharding import PartitionSpec as P

H = 16
FD = 16
NORM_FLOOR = 0.0001
LANES = 128
BF = jnp.bfloat16
F32 = jnp.float32
LIN = 128
FAR = 144
ONE = 152
LIVE_ROWS = 153

NN = (((1,), (0,)), ((), ()))
NT = (((1,), (1,)), ((), ()))
TN = (((0,), (0,)), ((), ()))


def dot(a, b, dims=NN, precision=None):
    return lax.dot_general(a, b, dims, preferred_element_type=F32, precision=precision)


def iota(shape, axis):
    return lax.broadcasted_iota(jnp.int32, shape, axis)


def features(t, rows, weights):
    diag, off, lin = weights
    tokens = t.shape[1]
    blocks = [t * t * diag if diag != 1.0 else t * t]
    scaled = t * off if off != 1.0 else t
    for o in range(1, FD // 2):
        blocks.append(scaled * pltpu.roll(t, FD - o, 0))
    blocks.append(t * lin if lin != 1.0 else t)
    blocks.append(scaled[: FD // 2] * t[FD // 2 :])
    blocks.append((iota((rows - ONE, tokens), 0) == 0).astype(F32))
    return jnp.concatenate(blocks, axis=0)


def pick_matrix(first_row, count, rows):
    r = iota((count, rows), 0) + first_row
    c = iota((count, rows), 1)
    i, j = r >> 4, r & 15
    o = (j - i) & 15
    place = jnp.where(
        o < 8, o * FD + i, jnp.where(o == 8, FAR + jnp.minimum(i, j), (FD - o) * FD + j)
    )
    return (place == c)


def kernel(cfg, len_ref, x_hbm, wq_hbm, wk_hbm, wv_hbm,
           mixed, quad_out, low_out, nq_out, nl_out,
           hid, wqk, wv, qs, ks, vs, nd, part, mgot, bsend, got, presend, prer, fwd, pre, tot,
           tsend, sqsend, sqgot, ztsend, ztgot,
           in_sem, s0, r0, s1, r1, s2, r2, s3, r3, s4, r4, s5, r5, s6, r6, s7, r7, s8, r8):
    n, nf, npr, span, heads, rows, sub = cfg
    me, fi = lax.axis_index("seq"), lax.axis_index("feat")
    own = heads * FD
    outer_n = n // 2
    zo, yi = me // 2, lax.rem(me, 2)
    mate = me + 1 - 2 * yi
    zpeer = 2 * lax.rem(zo + 1, outer_n) + yi
    head_dim = vs.shape[2] // heads

    base = pl.multiple_of((fi * own // LANES) * LANES, LANES)
    loads = [
        pltpu.make_async_copy(wq_hbm.at[:, pl.ds(base, LANES)], wqk.at[:, pl.ds(0, LANES)], in_sem.at[npr]),
        pltpu.make_async_copy(wk_hbm.at[:, pl.ds(base, LANES)], wqk.at[:, pl.ds(LANES, LANES)], in_sem.at[npr + 1]),
        pltpu.make_async_copy(wv_hbm, wv, in_sem.at[npr + 2]),
    ]
    last = outer_n - 1

    def hid_copy(p):
        return pltpu.make_async_copy(x_hbm.at[p], hid.at[p], in_sem.at[p])

    loads[0].start()
    loads[1].start()
    hid_copy(0).start()
    loads[2].start()
    for step in range(1, npr):
        hid_copy(step).start()

    barrier = pltpu.get_barrier_semaphore()

    @pl.loop(1, n)
    def _(i):
        pl.semaphore_signal(barrier, 1, device_id={"seq": lax.rem(me + i, n)}, device_id_type=pl.DeviceIdType.MESH)

    for i in range(1, nf):
        pl.semaphore_signal(barrier, 1, device_id={"feat": lax.rem(fi + i, nf)}, device_id_type=pl.DeviceIdType.MESH)
    pl.semaphore_wait(barrier, n - 1 + nf - 1)

    def to_seq(src, dst, ssem, rsem, target):
        return pltpu.make_async_remote_copy(
            src_ref=src, dst_ref=dst, send_sem=ssem, recv_sem=rsem,
            device_id={"seq": target}, device_id_type=pl.DeviceIdType.MESH)

    def to_feat(src, dst, ssem, rsem, target):
        return pltpu.make_async_remote_copy(
            src_ref=src, dst_ref=dst, send_sem=ssem, recv_sem=rsem,
            device_id={"feat": target}, device_id_type=pl.DeviceIdType.MESH)

    peer = lax.rem(me + 1, n)
    fpeer = lax.rem(fi + 1, nf)
    for load in loads:
        load.wait()

    def live_row(p):
        return ((iota((1, span), 1) + me * span) < len_ref[p]).astype(F32)

    def own_half(block):
        out = block[:, :own]
        for r in range(1, LANES // own):
            out = jnp.where(lax.rem(fi, LANES // own) == r, block[:, r * own:(r + 1) * own], out)
        return out

    def project(p, _):
        hid_copy(p).wait()
        x = hid[p]
        qk = dot(x, wqk[...])
        q = own_half(qk[:, :LANES]).astype(BF)
        k = own_half(qk[:, LANES:]).astype(BF)
        qs[p] = q
        ks[p] = k
        v = dot(x, wv[...]).astype(BF)
        vs[p] = v
        kt = k.astype(F32).T
        live = live_row(p)
        sums = []
        tail = rows - ONE
        row = iota((tail, LANES), 0)
        ones = jnp.ones((tail, span), BF)
        gap = jnp.zeros((tail, 2 * LANES - ONE - 8), F32)
        for h in range(heads):
            phi = (features(kt[h * FD:(h + 1) * FD], rows, (1.0, 1.0, 1.0)) * live).astype(BF)
            summed = dot(phi, v[:, h * head_dim:(h + 1) * head_dim])
            zh = dot(ones, phi, NT)
            more = jnp.concatenate([zh[:, LANES:ONE + 8], gap], axis=1)
            end = summed[ONE:] + jnp.where(row == 1, zh[:, :LANES], 0.0) + jnp.where(row == 2, more, 0.0)
            sums.append(jnp.concatenate([summed[:ONE], end], axis=0).astype(BF))
        half = heads // 2
        for c in range(2):
            part[p, c] = jnp.concatenate(sums[c * half:(c + 1) * half], axis=0).reshape(outer_n, sub, head_dim)
        to_seq(part.at[p, 1 - yi], mgot.at[p], s0.at[p], r0.at[p], mate).start()

        @pl.when(p > 0)
        def _():
            pair_up(p - 1)
        return 0

    def pair_up(p):
        to_seq(bsend.at[p], mgot.at[p], s0.at[p], r0.at[p], mate).wait_recv()
        bsend[p] = (part[p, yi].astype(F32) + mgot[p].astype(F32)).astype(BF)
        got[p, zo] = bsend[p, zo]

        @pl.loop(1, outer_n)
        def _(i):
            there = lax.rem(zo + i, outer_n)
            to_seq(bsend.at[p, there], got.at[p, zo], s1.at[p, i], r1.at[p, zo], 2 * there + yi).start()

    def home(p):
        def scan(z, acc):
            @pl.when(z != zo)
            def _():
                to_seq(bsend.at[p, z], got.at[p, z], s1.at[p, z], r1.at[p, z], zpeer).wait_recv()
            presend[p, z] = acc.astype(BF)
            return acc + got[p, z].astype(F32)

        total = lax.fori_loop(0, outer_n, scan, jnp.zeros((sub, head_dim), F32))
        tot[p, yi, zo] = total.astype(BF)
        prer[p, zo] = presend[p, zo]

        @pl.loop(1, outer_n)
        def _(i):
            there = lax.rem(zo + i, outer_n)

            @pl.when(there != 0)
            def _():
                to_seq(presend.at[p, there], prer.at[p, zo], s2.at[p, i], r2.at[p, zo], 2 * there + yi).start()

        @pl.loop(1, outer_n)
        def _(i):
            there = lax.rem(zo + i, outer_n)

            @pl.when(there != last)
            def _():
                to_seq(tot.at[p, yi, zo], tot.at[p, yi, zo], s3.at[p, i], r3.at[p, zo], 2 * there + yi).start()

    def take_prefix(p):
        @pl.when(zo != 0)
        def _():
            @pl.loop(1, outer_n)
            def _(i):
                there = lax.rem(zo + i, outer_n)
                to_seq(presend.at[p, there], prer.at[p, there], s2.at[p, i], r2.at[p, there], zpeer).wait_recv()

        @pl.when(zo == 0)
        def _():
            prer[p] = jnp.zeros(prer.shape[1:], BF)
        before = prer[p].astype(F32)
        fwd[p] = (before + jnp.where(yi == 0, part[p, yi].astype(F32), 0.0)).astype(BF)
        to_seq(fwd.at[p], pre.at[p, yi], s7.at[p], r7.at[p], mate).start()
        pre[p, yi] = (before + jnp.where(yi == 1, mgot[p].astype(F32), 0.0)).astype(BF)

    def take_total(p):
        @pl.when(zo != last)
        def _():
            @pl.loop(1, outer_n)
            def _(i):
                there = lax.rem(zo + i, outer_n)
                to_seq(presend.at[p, there], tot.at[p, yi, there], s3.at[p, i], r3.at[p, there], zpeer).wait_recv()
            to_seq(tot.at[p, yi], tot.at[p, yi], s8.at[p], r8.at[p], mate).start()

        @pl.when(zo == last)
        def _():
            @pl.loop(1, outer_n)
            def _(i):
                there = lax.rem(zo + i, outer_n)
                tot[p, yi, there] = (prer[p, there].astype(F32) + bsend[p, there].astype(F32)).astype(BF)
            to_seq(tot.at[p, yi], tot.at[p, yi], s8.at[p], r8.at[p], mate).start()

    lax.fori_loop(0, npr, project, 0)

    def inner(p, _):
        causal = iota((span, span), 0) >= iota((span, span), 1)
        keep = jnp.where(causal, live_row(p), 0.0)
        ones = jnp.ones((span, head_dim), BF)
        for h in range(heads):
            s = dot(qs[p, :, h * FD:(h + 1) * FD], ks[p, :, h * FD:(h + 1) * FD], NT)
            w = ((1.0 + s * (FD ** -0.5 + s * (0.5 / FD))) * keep).astype(BF)
            vv = jnp.concatenate([vs[p, :, h * head_dim:(h + 1) * head_dim], ones], axis=1)
            nd[p, h] = dot(w, vv)
        return 0

    sqsend[...] = jnp.zeros_like(sqsend)
    weights = (0.5 / FD, 1.0 / FD, FD ** -0.5)

    def joined(ref, p):
        return jnp.concatenate([ref[p, c].reshape(outer_n * sub, head_dim) for c in range(2)], axis=0)

    def zrow_of(state, h):
        block = state[h * rows + LIN:h * rows + ONE + 8].astype(F32)
        return jnp.concatenate([block[ONE + 1 - LIN:ONE + 2 - LIN], block[ONE + 2 - LIN:ONE + 3 - LIN, :ONE + 8 - LANES]], axis=1)

    def outer(p):
        to_seq(fwd.at[p], pre.at[p, 1 - yi], s7.at[p], r7.at[p], mate).wait_recv()
        qt = qs[p].astype(F32).T
        state = joined(pre, p)
        live = (iota((span, 1), 0) + me * span < len_ref[p]).astype(F32)
        earlier = jnp.minimum(me * span, len_ref[p]).astype(F32)
        sq = jnp.zeros((sqsend.shape[0], span), F32)
        for h in range(heads):
            phi = features(qt[h * FD:(h + 1) * FD], rows, weights).astype(BF)
            zr = zrow_of(state, h)
            zr = jnp.where(iota(zr.shape, 1) == ONE, 0.0, zr)
            zb = jnp.broadcast_to(zr, (head_dim, zr.shape[1])).astype(BF)
            phit = phi.T
            num = dot(phit, state[h * rows:(h + 1) * rows]) + nd[p, h, :, :head_dim]
            den = dot(phit[:, :zr.shape[1]], zb, NT) + nd[p, h, :, head_dim:] + earlier
            att = num / den * live
            nd[p, h, :, :head_dim] = att
            sq = sq + dot(jnp.ones((sqsend.shape[0], head_dim), BF), (att * att).astype(BF), NT)
        sqsend[...] = jnp.where(iota(sq.shape, 0) == p, sq, sqsend[...])

    ztsend[...] = jnp.zeros_like(ztsend)
    per = FD * FD // nf
    pick = pick_matrix(0, FD * FD, rows).astype(BF)

    def spread(p):
        to_seq(tot.at[p, yi], tot.at[p, 1 - yi], s8.at[p], r8.at[p], mate).wait_recv()
        state = joined(tot, p)
        zt = ztsend[...]
        zrow = iota(zt.shape, 0)
        for h in range(heads):
            mine = state[h * rows:(h + 1) * rows]
            zr = zrow_of(state, h)
            zr = jnp.where(iota(zr.shape, 1) == ONE, len_ref[p].astype(F32), zr)
            zt = jnp.where(zrow == p * heads + h, zr, zt)
            full = dot(pick, mine).astype(BF)
            for f in range(nf):
                tsend[f, p, h] = full[f * per:(f + 1) * per]
            tail = mine[LIN:].astype(F32)
            low_out[p, h] = jnp.concatenate(
                [tail[ONE - LIN:ONE - LIN + 1], tail[:FD] * FD ** -0.25], axis=0)
        ztsend[...] = zt
        for i in range(1, nf):
            target = lax.rem(fi + i, nf)
            to_feat(tsend.at[target, p], quad_out.at[fi, p], s5.at[i, p], r5.at[fi, p], target).start()

    lax.fori_loop(0, npr // 2, inner, 0)
    home(0)
    lax.fori_loop(npr // 2, npr, inner, 0)
    for p in range(1, npr - 2):
        home(p)
    for p in range(npr):
        if p == 0:
            pair_up(npr - 1)
        take_prefix(p)
        take_total(p)
        if p + npr - 2 < npr:
            home(p + npr - 2)
        if p > 0:
            outer(p - 1)
            spread(p - 1)
    outer(npr - 1)

    sqgot[fi] = sqsend[...]
    for i in range(1, nf):
        to_feat(sqsend, sqgot.at[fi], s4.at[i], r4.at[fi], lax.rem(fi + i, nf)).start()

    spread(npr - 1)
    zt = ztsend[...]
    ztgot[fi] = zt
    for i in range(1, nf):
        to_feat(ztsend, ztgot.at[fi], s6.at[i], r6.at[fi], lax.rem(fi + i, nf)).start()
    quad_out[fi] = tsend[fi]

    for i in range(1, nf):
        src = lax.rem(fi + i, nf)
        to_feat(sqsend, sqgot.at[src], s4.at[i], r4.at[src], fpeer).wait_recv()
    squares = sqgot[0]
    for f in range(1, nf):
        squares = squares + sqgot[f]
    width = nf * heads * head_dim
    mean = squares * (1.0 / width) + NORM_FLOOR
    inv = lax.rsqrt(mean)
    zsq = sqsend.shape[0]

    for p in range(npr):
        col = jnp.broadcast_to(inv[p:p + 1], (LANES, span)).T
        for h in range(heads):
            mixed[p, :, h * head_dim:(h + 1) * head_dim] = (nd[p, h, :, :head_dim] * col).astype(BF)

    for i in range(1, nf):
        src = lax.rem(fi + i, nf)
        to_feat(ztsend, ztgot.at[src], s6.at[i], r6.at[src], fpeer).wait_recv()
    own_pick = pick_matrix(fi * per, per, ONE + 8).astype(F32)
    for f in range(nf):
        nq = dot(ztgot[f], own_pick, NT, lax.Precision.HIGHEST) * (2.0 * FD) ** -0.5
        for p in range(npr):
            nq_out[p, f * heads:(f + 1) * heads] = nq[p * heads:(p + 1) * heads]
    lr, lc = iota((FD + 1, ONE + 8), 0), iota((FD + 1, ONE + 8), 1)
    low_pick = jnp.where(lr == 0, (lc == ONE).astype(F32), (lc == LIN - 1 + lr).astype(F32) * FD ** -0.25)
    nl = dot(ztgot[fi], low_pick, NT, lax.Precision.HIGHEST)
    for p in range(npr):
        nl_out[p] = nl[p * heads:(p + 1) * heads]

    for i in range(1, nf):
        src = lax.rem(fi + i, nf)

        @pl.loop(0, npr)
        def _(p):
            to_feat(tsend.at[src, p], quad_out.at[src, p], s5.at[i, p], r5.at[src, p], fpeer).wait_recv()
            to_feat(tsend.at[src, p], quad_out.at[src, p], s5.at[i, p], r5.at[src, p], fpeer).wait_send()
        to_feat(sqsend, sqgot.at[fi], s4.at[i], r4.at[fi], fpeer).wait_send()
        to_feat(ztsend, ztgot.at[fi], s6.at[i], r6.at[fi], fpeer).wait_send()

    @pl.loop(0, npr)
    def _(p):
        to_seq(part.at[p, yi], mgot.at[p], s0.at[p], r0.at[p], mate).wait_send()
        to_seq(fwd.at[p], pre.at[p, yi], s7.at[p], r7.at[p], mate).wait_send()
        to_seq(tot.at[p, yi], tot.at[p, yi], s8.at[p], r8.at[p], mate).wait_send()

        @pl.loop(1, outer_n)
        def _(i):
            there = lax.rem(zo + i, outer_n)
            to_seq(bsend.at[p, there], got.at[p, zo], s1.at[p, i], r1.at[p, zo], zpeer).wait_send()

            @pl.when(there != 0)
            def _():
                to_seq(presend.at[p, there], prer.at[p, zo], s2.at[p, i], r2.at[p, zo], zpeer).wait_send()

            @pl.when(there != last)
            def _():
                to_seq(tot.at[p, yi, zo], tot.at[p, yi, zo], s3.at[p, i], r3.at[p, zo], zpeer).wait_send()


def finish(cfg, own_ref, mixed, quad, low, nq, nl, mixed_out, quad_out, low_out, nq_out, nl_out):
    nf, heads = cfg
    mixed_out[...] = mixed[...]
    count = nq.shape[0]
    for b in range(count):
        mask = (own_ref[pl.program_id(0) * count + b] == lax.axis_index("seq")).astype(F32)
        finish_one(nf, heads, b, mask, quad, low, nq, nl, quad_out, low_out, nq_out, nl_out)


def finish_one(nf, heads, b, mask, quad, low, nq, nl, quad_out, low_out, nq_out, nl_out):
    for f in range(nf):
        quad_out[b, f * heads:(f + 1) * heads] = quad[f, b].astype(F32) * (mask * (2.0 * FD) ** -0.5)
    for h in range(heads):
        low_out[b, :, h, :] = low[b, h] * mask
    nq_out[b] = nq[b] * mask
    nl_out[b] = nl[b] * mask


def body(hidden_in, w_query, w_key, w_value, lengths, owners):
    npr, span, width = hidden_in.shape
    n, nf = lax.axis_size("seq"), lax.axis_size("feat")
    heads = H // nf
    head_dim = width // H
    step = 16 * n // heads
    rows = -(-LIVE_ROWS // 8) * 8
    rows = -(-rows // step) * step
    sub = heads * rows // n
    cfg = (n, nf, npr, span, heads, rows, sub)
    per = FD * FD // nf
    dma = pltpu.SemaphoreType.DMA
    vm = pltpu.VMEM
    ph = npr * heads
    out = pl.pallas_call(
        functools.partial(kernel, cfg),
        out_shape=(
            jax.ShapeDtypeStruct((npr, span, heads * head_dim), BF),
            jax.ShapeDtypeStruct((nf, npr, heads, per, head_dim), BF),
            jax.ShapeDtypeStruct((npr, heads, FD + 1, head_dim), F32),
            jax.ShapeDtypeStruct((npr, H, per), F32),
            jax.ShapeDtypeStruct((npr, heads, FD + 1), F32),
        ),
        in_specs=[pl.BlockSpec(memory_space=pltpu.SMEM)] + [pl.BlockSpec(memory_space=pl.ANY)] * 4,
        out_specs=[pl.BlockSpec(memory_space=pltpu.VMEM)] * 5,
        scratch_shapes=[
            vm((npr, span, width), BF),
            vm((width, 2 * LANES), BF),
            vm((width, heads * head_dim), BF),
            vm((npr, span, heads * FD), BF),
            vm((npr, span, heads * FD), BF),
            vm((npr, span, heads * head_dim), BF),
            vm((npr, heads, span, 2 * head_dim), F32),
            vm((npr, 2, n // 2, sub, head_dim), BF),
            vm((npr, n // 2, sub, head_dim), BF),
            vm((npr, n // 2, sub, head_dim), BF),
            vm((npr, n // 2, sub, head_dim), BF),
            vm((npr, n // 2, sub, head_dim), BF),
            vm((npr, n // 2, sub, head_dim), BF),
            vm((npr, n // 2, sub, head_dim), BF),
            vm((npr, 2, n // 2, sub, head_dim), BF),
            vm((npr, 2, n // 2, sub, head_dim), BF),
            vm((nf, npr, heads, per, head_dim), BF),
            vm((8, span), F32),
            vm((nf, 8, span), F32),
            vm((ph, ONE + 8), F32),
            vm((nf, ph, ONE + 8), F32),
            dma((npr + 3,)),
            dma((npr,)), dma((npr,)), dma((npr, n // 2)), dma((npr, n // 2)),
            dma((npr, n // 2)), dma((npr, n // 2)), dma((npr, n // 2)), dma((npr, n // 2)),
            dma((nf,)), dma((nf,)), dma((nf, npr)), dma((nf, npr)), dma((nf,)), dma((nf,)),
            dma((npr,)), dma((npr,)), dma((npr,)), dma((npr,)),
        ],
        compiler_params=pltpu.CompilerParams(
            collective_id=0, has_side_effects=True, vmem_limit_bytes=56 * 1024 * 1024
        ),
        name="layer",
    )(lengths, hidden_in, w_query, w_key, w_value)
    mixed, quad, low, nq, nl = out
    block = pl.BlockSpec
    group = 2 - npr % 2
    mixed, quad, low, nq, nl = pl.pallas_call(
        functools.partial(finish, (nf, heads)),
        grid=(npr // group,),
        out_shape=(
            jax.ShapeDtypeStruct(mixed.shape, BF),
            jax.ShapeDtypeStruct((npr, H, per, head_dim), F32),
            jax.ShapeDtypeStruct((npr, FD + 1, heads, head_dim), F32),
            jax.ShapeDtypeStruct(nq.shape, F32),
            jax.ShapeDtypeStruct(nl.shape, F32),
        ),
        in_specs=[
            block(memory_space=pltpu.SMEM),
            block((group, span, heads * head_dim), lambda p: (p, 0, 0)),
            block((nf, group, heads, per, head_dim), lambda p: (0, p, 0, 0, 0)),
            block((group, heads, FD + 1, head_dim), lambda p: (p, 0, 0, 0)),
            block((group, H, per), lambda p: (p, 0, 0)),
            block((group, heads, FD + 1), lambda p: (p, 0, 0)),
        ],
        out_specs=[
            block((group, span, heads * head_dim), lambda p: (p, 0, 0)),
            block((group, H, per, head_dim), lambda p: (p, 0, 0, 0)),
            block((group, FD + 1, heads, head_dim), lambda p: (p, 0, 0, 0)),
            block((group, H, per), lambda p: (p, 0, 0)),
            block((group, heads, FD + 1), lambda p: (p, 0, 0)),
        ],
        name="finish",
    )(owners, mixed, quad, low, nq, nl)
    return (mixed, quad[None], jnp.transpose(low, (0, 2, 1, 3))[None], nq[None], nl[None])


def solution(mesh):
    placed = (P(None, "seq", None), P(), P(), P(None, "feat"), P(), P())
    return jax.shard_map(
        body,
        mesh=mesh,
        in_specs=placed,
        out_specs=(
            P(None, "seq", "feat"),
            P("seq", None, None, "feat", None),
            P("seq", None, "feat", None, None),
            P("seq", None, None, "feat"),
            P("seq", None, "feat", None),
        ),
        check_vma=False,
    )
```

profile of v0, /device:TPU:0, one launch (start us, length us, event | category | flops | bytes accessed | tf_op | source)
XLA Modules:
  0.0 49.4 jit_solution(2440701114116534388)
XLA Ops:
  0.6 45.6 %layer.1 = (bf16[4,256,512]{2,1,0:T(8,128)(2,1)}, bf16[4,4,4,64,128]{4,3,2,1,0:T(8,128)(2,1)}, f32[4,4,17,128]{3,2,1,0:T(8,128)}, f32[4,16,64]{2,1,0:T(8,128)}, f32[4,4,17]{2,1,0:T(4,128)}) custom-call(s32[4]{0:T(128)} %len_ref.1, bf16[4,256,2048]{2,1,0:T(8,128)(2,1)} %x_hbm.1, bf16[2048,256]{1,0:T(8,128)(2,1)} %wq_hbm.1, bf16[2048,256]{1,0:T(8,128)(2,1)} %wk_hbm.1, ...), custom_call_target="tpu_custom_call" | custom-call | tf_op jit(solution)/shard_map/layer/pallas_call | solution.py:417
  46.3 3.1 %finish.1 = (bf16[4,256,512]{2,1,0:T(8,128)(2,1)}, f32[4,16,64,128]{3,2,1,0:T(8,128)}, f32[4,17,4,128]{3,2,1,0:T(4,128)}, f32[4,16,64]{2,1,0:T(8,128)}, f32[4,4,17]{2,1,0:T(4,128)}) custom-call(s32[4]{0:T(128)} %own_ref.1, bf16[4,256,512]{2,1,0:T(8,128)(2,1)} %get-tuple-element.15.mixed, bf16[4,4,4,64,128]{4,3,2,1,0:T(8,128)(2,1)} %get-tuple-element.16.quad, ...), custom_call_target="tpu_custom_call" | custom-call | tf_op jit(solution)/shard_map/finish/pallas_call | solution.py:464
where the time goes:
time: 49.5 us; the launch traced here: 49.4 us
  Pallas kernels  48.7 us (98%)
  between operations  0.64 us (1%)
    pallas_call x1, Pallas kernels, body(): pl.pallas_call(functools.partial(kernel, cfg), out_shape=(jax.ShapeDtypeS...  45.6 us
    pallas_call x1, Pallas kernels, body(): pl.pallas_call(functools.partial(finish, (nf, heads)), grid=(npr // group...  3.07 us

commit v1 on v0

--- a/solution.py
+++ b/solution.py
@@ -56,9 +56,9 @@
 
 
 def kernel(cfg, len_ref, x_hbm, wq_hbm, wk_hbm, wv_hbm,
-           mixed, quad_out, low_out, nq_out, nl_out,
+           att_out, sqgot, quad_out, low_out, ztgot,
            hid, wqk, wv, qs, ks, vs, nd, part, mgot, bsend, got, presend, prer, fwd, pre, tot,
-           tsend, sqsend, sqgot, ztsend, ztgot,
+           tsend, sqsend, ztsend,
            in_sem, s0, r0, s1, r1, s2, r2, s3, r3, s4, r4, s5, r5, s6, r6, s7, r7, s8, r8):
     n, nf, npr, span, heads, rows, sub = cfg
     me, fi = lax.axis_index("seq"), lax.axis_index("feat")
@@ -95,7 +95,6 @@
 
     for i in range(1, nf):
         pl.semaphore_signal(barrier, 1, device_id={"feat": lax.rem(fi + i, nf)}, device_id_type=pl.DeviceIdType.MESH)
-    pl.semaphore_wait(barrier, n - 1 + nf - 1)
 
     def to_seq(src, dst, ssem, rsem, target):
         return pltpu.make_async_remote_copy(
@@ -148,6 +147,10 @@
         half = heads // 2
         for c in range(2):
             part[p, c] = jnp.concatenate(sums[c * half:(c + 1) * half], axis=0).reshape(outer_n, sub, head_dim)
+
+        @pl.when(p == 0)
+        def _():
+            pl.semaphore_wait(barrier, n - 1 + nf - 1)
         to_seq(part.at[p, 1 - yi], mgot.at[p], s0.at[p], r0.at[p], mate).start()
 
         @pl.when(p > 0)
@@ -265,7 +268,7 @@
             num = dot(phit, state[h * rows:(h + 1) * rows]) + nd[p, h, :, :head_dim]
             den = dot(phit[:, :zr.shape[1]], zb, NT) + nd[p, h, :, head_dim:] + earlier
             att = num / den * live
-            nd[p, h, :, :head_dim] = att
+            att_out[p, :, h * head_dim:(h + 1) * head_dim] = att
             sq = sq + dot(jnp.ones((sqsend.shape[0], head_dim), BF), (att * att).astype(BF), NT)
         sqsend[...] = jnp.where(iota(sq.shape, 0) == p, sq, sqsend[...])
 
@@ -325,33 +328,9 @@
     for i in range(1, nf):
         src = lax.rem(fi + i, nf)
         to_feat(sqsend, sqgot.at[src], s4.at[i], r4.at[src], fpeer).wait_recv()
-    squares = sqgot[0]
-    for f in range(1, nf):
-        squares = squares + sqgot[f]
-    width = nf * heads * head_dim
-    mean = squares * (1.0 / width) + NORM_FLOOR
-    inv = lax.rsqrt(mean)
-    zsq = sqsend.shape[0]
-
-    for p in range(npr):
-        col = jnp.broadcast_to(inv[p:p + 1], (LANES, span)).T
-        for h in range(heads):
-            mixed[p, :, h * head_dim:(h + 1) * head_dim] = (nd[p, h, :, :head_dim] * col).astype(BF)
-
     for i in range(1, nf):
         src = lax.rem(fi + i, nf)
         to_feat(ztsend, ztgot.at[src], s6.at[i], r6.at[src], fpeer).wait_recv()
-    own_pick = pick_matrix(fi * per, per, ONE + 8).astype(F32)
-    for f in range(nf):
-        nq = dot(ztgot[f], own_pick, NT, lax.Precision.HIGHEST) * (2.0 * FD) ** -0.5
-        for p in range(npr):
-            nq_out[p, f * heads:(f + 1) * heads] = nq[p * heads:(p + 1) * heads]
-    lr, lc = iota((FD + 1, ONE + 8), 0), iota((FD + 1, ONE + 8), 1)
-    low_pick = jnp.where(lr == 0, (lc == ONE).astype(F32), (lc == LIN - 1 + lr).astype(F32) * FD ** -0.25)
-    nl = dot(ztgot[fi], low_pick, NT, lax.Precision.HIGHEST)
-    for p in range(npr):
-        nl_out[p] = nl[p * heads:(p + 1) * heads]
-
     for i in range(1, nf):
         src = lax.rem(fi + i, nf)
 
@@ -382,22 +361,43 @@
                 to_seq(tot.at[p, yi, zo], tot.at[p, yi, zo], s3.at[p, i], r3.at[p, zo], zpeer).wait_send()
 
 
-def finish(cfg, own_ref, mixed, quad, low, nq, nl, mixed_out, quad_out, low_out, nq_out, nl_out):
-    nf, heads = cfg
-    mixed_out[...] = mixed[...]
-    count = nq.shape[0]
-    for b in range(count):
-        mask = (own_ref[pl.program_id(0) * count + b] == lax.axis_index("seq")).astype(F32)
-        finish_one(nf, heads, b, mask, quad, low, nq, nl, quad_out, low_out, nq_out, nl_out)
-
-
-def finish_one(nf, heads, b, mask, quad, low, nq, nl, quad_out, low_out, nq_out, nl_out):
+def finish(cfg, own_ref, att, sq, quad, low, zt, mixed_out, quad_out, low_out, nq_out, nl_out,
+           mixed_buf, quad_buf, sem):
+    nf, heads, npr, per = cfg
+    span, width = att.shape[1], att.shape[2]
+    fi, me = lax.axis_index("feat"), lax.axis_index("seq")
+    squares = sq[0]
+    for f in range(1, nf):
+        squares = squares + sq[f]
+    inv = lax.rsqrt(squares * (1.0 / (nf * width)) + NORM_FLOOR)
+    writes = []
+    for p in range(npr):
+        mask = (own_ref[p] == me).astype(F32)
+        for f in range(nf):
+            quad_buf[p, f * heads:(f + 1) * heads] = quad[f, p].astype(F32) * (mask * (2.0 * FD) ** -0.5)
+        writes.append(pltpu.make_async_copy(quad_buf.at[p], quad_out.at[p], sem.at[0, p]))
+        writes[-1].start()
+        col = jnp.broadcast_to(inv[p:p + 1], (LANES, span)).T
+        for c in range(width // LANES):
+            mixed_buf[p, :, c * LANES:(c + 1) * LANES] = (att[p, :, c * LANES:(c + 1) * LANES] * col).astype(BF)
+        writes.append(pltpu.make_async_copy(mixed_buf.at[p], mixed_out.at[p], sem.at[1, p]))
+        writes[-1].start()
+    own_pick = pick_matrix(fi * per, per, ONE + 8).astype(F32)
+    lr, lc = iota((FD + 1, ONE + 8), 0), iota((FD + 1, ONE + 8), 1)
+    low_pick = jnp.where(lr == 0, (lc == ONE).astype(F32), (lc == LIN - 1 + lr).astype(F32) * FD ** -0.25)
+    nl = dot(zt[fi], low_pick, NT, lax.Precision.HIGHEST)
     for f in range(nf):
-        quad_out[b, f * heads:(f + 1) * heads] = quad[f, b].astype(F32) * (mask * (2.0 * FD) ** -0.5)
-    for h in range(heads):
-        low_out[b, :, h, :] = low[b, h] * mask
-    nq_out[b] = nq[b] * mask
-    nl_out[b] = nl[b] * mask
+        nq = dot(zt[f], own_pick, NT, lax.Precision.HIGHEST) * (2.0 * FD) ** -0.5
+        for p in range(npr):
+            mask = (own_ref[p] == me).astype(F32)
+            nq_out[p, f * heads:(f + 1) * heads] = nq[p * heads:(p + 1) * heads] * mask
+    for p in range(npr):
+        mask = (own_ref[p] == me).astype(F32)
+        nl_out[p] = nl[p * heads:(p + 1) * heads] * mask
+        for h in range(heads):
+            low_out[p, :, h, :] = low[p, h] * mask
+    for write in writes:
+        write.wait()
 
 
 def body(hidden_in, w_query, w_key, w_value, lengths, owners):
@@ -417,13 +417,13 @@
     out = pl.pallas_call(
         functools.partial(kernel, cfg),
         out_shape=(
-            jax.ShapeDtypeStruct((npr, span, heads * head_dim), BF),
-            jax.ShapeDtypeStruct((nf, npr, heads, per, head_dim), BF),
-            jax.ShapeDtypeStruct((npr, heads, FD + 1, head_dim), F32),
-            jax.ShapeDtypeStruct((npr, H, per), F32),
-            jax.ShapeDtypeStruct((npr, heads, FD + 1), F32),
+            vm((npr, span, heads * head_dim), F32),
+            vm((nf, 8, span), F32),
+            vm((nf, npr, heads, per, head_dim), BF),
+            vm((npr, heads, FD + 1, head_dim), F32),
+            vm((nf, ph, ONE + 8), F32),
         ),
-        in_specs=[pl.BlockSpec(memory_space=pltpu.SMEM)] + [pl.BlockSpec(memory_space=pl.ANY)] * 4,
+        in_specs=[pl.BlockSpec(memory_space=pltpu.SMEM)] + [pl.BlockSpec(memory_space=pltpu.HBM)] * 4,
         out_specs=[pl.BlockSpec(memory_space=pltpu.VMEM)] * 5,
         scratch_shapes=[
             vm((npr, span, width), BF),
@@ -444,9 +444,7 @@
             vm((npr, 2, n // 2, sub, head_dim), BF),
             vm((nf, npr, heads, per, head_dim), BF),
             vm((8, span), F32),
-            vm((nf, 8, span), F32),
             vm((ph, ONE + 8), F32),
-            vm((nf, ph, ONE + 8), F32),
             dma((npr + 3,)),
             dma((npr,)), dma((npr,)), dma((npr, n // 2)), dma((npr, n // 2)),
             dma((npr, n // 2)), dma((npr, n // 2)), dma((npr, n // 2)), dma((npr, n // 2)),
@@ -454,40 +452,31 @@
             dma((npr,)), dma((npr,)), dma((npr,)), dma((npr,)),
         ],
         compiler_params=pltpu.CompilerParams(
-            collective_id=0, has_side_effects=True, vmem_limit_bytes=56 * 1024 * 1024
+            collective_id=0, has_side_effects=True, vmem_limit_bytes=40 * 1024 * 1024
         ),
         name="layer",
-    )(lengths, hidden_in, w_query, w_key, w_value)
-    mixed, quad, low, nq, nl = out
+    )(lengths, *[pltpu.with_memory_space_constraint(a, pltpu.HBM) for a in (hidden_in, w_query, w_key, w_value)])
+    onchip = [pltpu.with_memory_space_constraint(o, pltpu.VMEM) for o in out]
     block = pl.BlockSpec
-    group = 2 - npr % 2
     mixed, quad, low, nq, nl = pl.pallas_call(
-        functools.partial(finish, (nf, heads)),
-        grid=(npr // group,),
+        functools.partial(finish, (nf, heads, npr, per)),
         out_shape=(
-            jax.ShapeDtypeStruct(mixed.shape, BF),
+            jax.ShapeDtypeStruct((npr, span, heads * head_dim), BF),
             jax.ShapeDtypeStruct((npr, H, per, head_dim), F32),
             jax.ShapeDtypeStruct((npr, FD + 1, heads, head_dim), F32),
-            jax.ShapeDtypeStruct(nq.shape, F32),
-            jax.ShapeDtypeStruct(nl.shape, F32),
+            jax.ShapeDtypeStruct((npr, H, per), F32),
+            jax.ShapeDtypeStruct((npr, heads, FD + 1), F32),
         ),
-        in_specs=[
-            block(memory_space=pltpu.SMEM),
-            block((group, span, heads * head_dim), lambda p: (p, 0, 0)),
-            block((nf, group, heads, per, head_dim), lambda p: (0, p, 0, 0, 0)),
-            block((group, heads, FD + 1, head_dim), lambda p: (p, 0, 0, 0)),
-            block((group, H, per), lambda p: (p, 0, 0)),
-            block((group, heads, FD + 1), lambda p: (p, 0, 0)),
+        in_specs=[block(memory_space=pltpu.SMEM)] + [block(memory_space=pltpu.VMEM)] * 5,
+        out_specs=[block(memory_space=pl.ANY)] * 2 + [block(memory_space=pltpu.VMEM)] * 3,
+        scratch_shapes=[
+            vm((npr, span, heads * head_dim), BF),
+            vm((npr, H, per, head_dim), F32),
+            dma((2, npr)),
         ],
-        out_specs=[
-            block((group, span, heads * head_dim), lambda p: (p, 0, 0)),
-            block((group, H, per, head_dim), lambda p: (p, 0, 0, 0)),
-            block((group, FD + 1, heads, head_dim), lambda p: (p, 0, 0, 0)),
-            block((group, H, per), lambda p: (p, 0, 0)),
-            block((group, heads, FD + 1), lambda p: (p, 0, 0)),
-        ],
+        compiler_params=pltpu.CompilerParams(vmem_limit_bytes=16 * 1024 * 1024),
         name="finish",
-    )(owners, mixed, quad, low, nq, nl)
+    )(owners, *onchip)
     return (mixed, quad[None], jnp.transpose(low, (0, 2, 1, 3))[None], nq[None], nl[None])
 
 

time: 49.5 us -> 48.3 us (0.976)
  Pallas kernels: 48.7 us -> 46.8 us
  local copies, waits for them, and re-layouts: 0 us -> 0.65 us
    pallas_call x2, Pallas kernels: 48.7 us -> 46.8 us  [the longest x1 43.6 us: body(): pl.pallas_call(functools.partial(kernel, cfg), out_shape=(vm((npr, span,...]
    unnamed x0 -> x4, local copies, waits for them, and re-layouts: none -> 0.65 us
where the time goes in v1:
time: 48.3 us; the launch traced here: 48.1 us
  Pallas kernels  46.8 us (97%)
  between operations  0.66 us (1%)
  local copies, waits for them, and re-layouts  0.65 us (1%)
    pallas_call x1, Pallas kernels, body(): pl.pallas_call(functools.partial(kernel, cfg), out_shape=(vm((npr, span,...  43.6 us
    pallas_call x1, Pallas kernels, body(): pl.pallas_call(functools.partial(finish, (nf, heads, npr, per)), out_shap...  3.24 us

profile of v1, /device:TPU:0, one launch (start us, length us, event | category | flops | bytes accessed | tf_op | source)
XLA Modules:
  0.0 48.1 jit_solution(14638021455096944142)
XLA Ops:
  0.6 0.0 copy-start
  0.6 0.6 %copy-done = s32[4]{0:T(128)S(1)} copy-done((s32[4]{0:T(128)S(1)}, s32[4]{0:T(128)}, u32[]{:S(2)}) %copy-start) | copy-done | bytes 40
  1.3 0.0 copy-start.1
  1.3 43.6 %layer.1 = (f32[4,256,512]{2,1,0:T(8,128)S(1)}, f32[4,8,256]{2,1,0:T(8,128)S(1)}, bf16[4,4,4,64,128]{4,3,2,1,0:T(8,128)(2,1)S(1)}, f32[4,4,17,128]{3,2,1,0:T(8,128)S(1)}, f32[4,16,160]{2,1,0:T(8,128)S(1)}) custom-call(s32[4]{0:T(128)S(1)} %copy-done, bf16[4,256,2048]{2,1,0:T(8,128)(2,1)} %x_hbm.1, bf16[2048,256]{1,0:T(8,128)(2,1)} %wq_hbm.1, ...), custom_call_target="tpu_custom_call" | custom-call | tf_op jit(solution)/shard_map/layer/pallas_call | solution.py:417
  44.9 0.0 copy-done.1
  44.9 3.2 %finish.1 = (bf16[4,256,512]{2,1,0:T(8,128)(2,1)}, f32[4,16,64,128]{3,2,1,0:T(8,128)}, f32[4,17,4,128]{3,2,1,0:T(4,128)}, f32[4,16,64]{2,1,0:T(8,128)}, f32[4,4,17]{2,1,0:T(4,128)}) custom-call(s32[4]{0:T(128)S(1)} %copy-done.1, f32[4,256,512]{2,1,0:T(8,128)S(1)} %get-tuple-element.15.att, f32[4,8,256]{2,1,0:T(8,128)S(1)} %get-tuple-element.16.sq, ...), custom_call_target="tpu_custom_call" | custom-call | tf_op jit(solution)/shard_map/finish/pallas_call | solution.py:461
Async XLA Ops:
  0.6 0.7 %copy-start = (s32[4]{0:T(128)S(1)}, s32[4]{0:T(128)}, u32[]{:S(2)}) copy-start(s32[4]{0:T(128)} %len_ref.1) | copy-start | bytes 52
  1.3 43.6 %copy-start.1 = (s32[4]{0:T(128)S(1)}, s32[4]{0:T(128)}, u32[]{:S(2)}) copy-start(s32[4]{0:T(128)} %own_ref.1) | copy-start | bytes 52

commit v2 on v1

v2 whole, which is shorter than its diff:
```python
import functools

import jax
import jax.numpy as jnp
from jax import lax
from jax.experimental import pallas as pl
from jax.experimental.pallas import tpu as pltpu
from jax.sharding import PartitionSpec as P

H = 16
FD = 16
NORM_FLOOR = 0.0001
LANES = 128
BF = jnp.bfloat16
F32 = jnp.float32
LIN = 128
FAR = 144
ONE = 152
LIVE_ROWS = 153

NN = (((1,), (0,)), ((), ()))
NT = (((1,), (1,)), ((), ()))
TN = (((0,), (0,)), ((), ()))


def dot(a, b, dims=NN, precision=None):
    return lax.dot_general(a, b, dims, preferred_element_type=F32, precision=precision)


def iota(shape, axis):
    return lax.broadcasted_iota(jnp.int32, shape, axis)


def features(t, rows, weights):
    diag, off, lin = weights
    tokens = t.shape[1]
    blocks = [t * t * diag if diag != 1.0 else t * t]
    scaled = t * off if off != 1.0 else t
    for o in range(1, FD // 2):
        blocks.append(scaled * pltpu.roll(t, FD - o, 0))
    blocks.append(t * lin if lin != 1.0 else t)
    blocks.append(scaled[: FD // 2] * t[FD // 2 :])
    blocks.append((iota((rows - ONE, tokens), 0) == 0).astype(F32))
    return jnp.concatenate(blocks, axis=0)


def pick_matrix(first_row, count, rows):
    r = iota((count, rows), 0) + first_row
    c = iota((count, rows), 1)
    i, j = r >> 4, r & 15
    o = (j - i) & 15
    place = jnp.where(
        o < 8, o * FD + i, jnp.where(o == 8, FAR + jnp.minimum(i, j), (FD - o) * FD + j)
    )
    return (place == c)


def kernel(cfg, len_hbm, own_hbm, x_hbm, wq_hbm, wk_hbm, wv_hbm,
           att_out, sqgot, quad_out, low_out, ztgot, mine_out,
           hid, wall, qs, ks, vs, kt, phs, nd, part, mgot, bsum, up_got, up_send, dn_got, dn_send,
           fwd, pre, bwd, suf, tsend, sqsend, ztsend, len_ref, own_ref,
           in_sem, s0, r0, s1, r1, s2, r2, s3, r3, s4, r4, s5, r5, s6, r6, s7, r7):
    n, nf, npr, span, heads, rows, cpp, lag, turn = cfg
    me, fi = lax.axis_index("seq"), lax.axis_index("feat")
    own = heads * FD
    half = heads // 2
    last = n // 2 - 1
    zo, yi = me // 2, lax.rem(me, 2)
    mate = me + 1 - 2 * yi
    head_dim = vs.shape[2] // heads
    spot = lax.rem(fi * own, LANES)
    hw = half * head_dim
    chunks = npr * cpp
    below, above = zo > 0, zo < last

    def half_cols(c):
        return pl.ds(pl.multiple_of(c * hw, LANES), hw)

    base = pl.multiple_of((fi * own // LANES) * LANES, LANES)
    qk_loads = [
        pltpu.make_async_copy(wq_hbm.at[:, pl.ds(base, LANES)], wall.at[:, pl.ds(0, LANES)], in_sem.at[npr]),
        pltpu.make_async_copy(wk_hbm.at[:, pl.ds(base, LANES)], wall.at[:, pl.ds(LANES, LANES)], in_sem.at[npr + 1]),
    ]

    def v_load(step):
        cols = half_cols(1 - yi if step == 0 else yi)
        return pltpu.make_async_copy(wv_hbm.at[:, cols], wall.at[:, pl.ds(2 * LANES + step * hw, hw)], in_sem.at[npr + 2 + step])

    def hid_copy(p):
        return pltpu.make_async_copy(x_hbm.at[p], hid.at[p], in_sem.at[p])

    for load in qk_loads:
        load.start()
    hid_copy(0).start()
    v_load(0).start()
    v_load(1).start()
    small = [
        pltpu.make_async_copy(len_hbm, len_ref, in_sem.at[npr + 4]),
        pltpu.make_async_copy(own_hbm, own_ref, in_sem.at[npr + 5]),
    ]
    for load in small:
        load.start()

    barrier = pltpu.get_barrier_semaphore()

    def greet(axis, target):
        pl.semaphore_signal(barrier, 1, device_id={axis: target}, device_id_type=pl.DeviceIdType.MESH)

    greet("seq", mate)

    @pl.when(below)
    def _():
        greet("seq", me - 2)

    @pl.when(above)
    def _():
        greet("seq", me + 2)

    for i in range(1, nf):
        greet("feat", lax.rem(fi + i, nf))

    @pl.when(zo == 0)
    def _():
        up_got[...] = jnp.zeros(up_got.shape, BF)

    @pl.when(zo == last)
    def _():
        dn_got[...] = jnp.zeros(dn_got.shape, BF)

    def to_seq(src, dst, ssem, rsem, target):
        return pltpu.make_async_remote_copy(
            src_ref=src, dst_ref=dst, send_sem=ssem, recv_sem=rsem,
            device_id={"seq": target}, device_id_type=pl.DeviceIdType.MESH)

    def to_feat(src, dst, ssem, rsem, target):
        return pltpu.make_async_remote_copy(
            src_ref=src, dst_ref=dst, send_sem=ssem, recv_sem=rsem,
            device_id={"feat": target}, device_id_type=pl.DeviceIdType.MESH)

    fpeer = lax.rem(fi + 1, nf)

    def swap_copy(p, j):
        return to_seq(part.at[p, 0, j], mgot.at[p, j], s0, r0.at[p, j], mate)

    def up_copy(p, j):
        return to_seq(up_send.at[p, j], up_got.at[p, j], s1, r1.at[p, j], me + 2 * above.astype(jnp.int32) - 2 * (1 - above.astype(jnp.int32)))

    def dn_copy(p, j):
        return to_seq(dn_send.at[p, j], dn_got.at[p, j], s2, r2.at[p, j], me - 2 * below.astype(jnp.int32) + 2 * (1 - below.astype(jnp.int32)))

    def pre_copy(p, j):
        return to_seq(fwd.at[p, j], pre.at[p, 0, j], s3, r3.at[p, j], mate)

    def suf_copy(p, j):
        return to_seq(bwd.at[p, j], suf.at[p, j], s7, r7.at[p, j], mate)

    def live_row(p):
        return ((iota((1, span), 1) + me * span) < len_ref[p]).astype(F32)

    tail = rows - ONE
    weights = (0.5 / FD, 1.0 / FD, FD ** -0.5)

    def sums_of(slot, side, v, live):
        row = iota((tail, LANES), 0)
        ones = jnp.ones((tail, span), BF)
        gap = jnp.zeros((tail, 2 * LANES - ONE - 8), F32)
        sums = []
        for h in range(half):
            phi = (features(kt[side, head_rows(slot + h)], rows, (1.0, 1.0, 1.0)) * live).astype(BF)
            summed = dot(phi, v[:, h * head_dim:(h + 1) * head_dim])
            zh = dot(ones, phi, NT)
            more = jnp.concatenate([zh[:, LANES:ONE + 8], gap], axis=1)
            end = summed[ONE:] + jnp.where(row == 1, zh[:, :LANES], 0.0) + jnp.where(row == 2, more, 0.0)
            sums.append(jnp.concatenate([summed[:ONE], end], axis=0).astype(BF))
        return jnp.concatenate(sums, axis=0).reshape(part.shape[2:])

    def head_of(slot):
        return (1 - yi if slot < half else yi) * half + slot % half

    def head_rows(slot):
        return pl.ds(pl.multiple_of(spot + head_of(slot) * FD, FD), FD)

    for load in qk_loads:
        load.wait()
    v_load(0).wait()
    for load in small:
        load.wait()
    hid_copy(0).wait()
    for p in range(1, npr):
        hid_copy(p).start()
    middle = wall.shape[0] // 2

    def project(p, first):
        if not first:
            hid_copy(p).wait()
        x = hid[p]
        head = dot(x, wall[:, :2 * LANES + hw])
        k = head[:, LANES:2 * LANES].astype(BF)
        qs[p] = head[:, :LANES].astype(BF)
        ks[p] = k
        slot = lax.rem(p, 2)
        kt[slot] = k.astype(F32).T
        v = head[:, 2 * LANES:].astype(BF)
        vs[p, :, :hw] = v
        if first:
            v_load(1).wait()
        else:
            late(p - 1)
        mine = dot(x[:, :middle], wall[:middle, 2 * LANES + hw:]) + dot(x[:, middle:], wall[middle:, 2 * LANES + hw:])
        part[p, 0] = sums_of(0, slot, v, live_row(p))
        vs[p, :, hw:] = mine.astype(BF)
        if first:
            pl.semaphore_wait(barrier, nf + below.astype(jnp.int32) + above.astype(jnp.int32))
        for j in range(cpp):
            swap_copy(p, j).start()

    def late(p):
        part[p, 1] = sums_of(half, lax.rem(p, 2), vs[p, :, hw:], live_row(p))

    def pair(k):
        p, j = k // cpp, lax.rem(k, cpp)
        swap_copy(p, j).wait_recv()
        bsum[p, j] = (part[p, 1, j].astype(F32) + mgot[p, j].astype(F32)).astype(BF)

    def take_up(k):
        p, j = k // cpp, lax.rem(k, cpp)

        @pl.when(below)
        def _():
            up_copy(p, j).wait_recv()
        before = up_got[p, j].astype(F32)

        @pl.when(above)
        def _():
            up_send[p, j] = (up_got[p, j].astype(F32) + bsum[p, j].astype(F32)).astype(BF)
            up_copy(p, j).start()
        fwd[p, j] = (before + jnp.where(yi == 0, part[p, 1, j].astype(F32), 0.0)).astype(BF)
        pre_copy(p, j).start()
        pre[p, 1, j] = (before + jnp.where(yi == 1, mgot[p, j].astype(F32), 0.0)).astype(BF)

    def take_down(k):
        p, j = k // cpp, lax.rem(k, cpp)

        @pl.when(above)
        def _():
            dn_copy(p, j).wait_recv()
        after = dn_got[p, j].astype(F32)

        @pl.when(below)
        def _():
            dn_send[p, j] = (dn_got[p, j].astype(F32) + bsum[p, j].astype(F32)).astype(BF)
            dn_copy(p, j).start()
        bwd[p, j] = (after + jnp.where(yi == 1, part[p, 1, j].astype(F32), 0.0)).astype(BF)
        suf_copy(p, j).start()

    def at(t, body, stride=1):
        @pl.when((t >= 0) & (t < chunks) & (lax.rem(t, stride) == 0))
        def _():
            body(t // stride)

    def chain(t):
        at(t, pair)
        at(t - lag * zo, take_up)
        at(t - lag * (last - zo), take_down)

    project(0, True)

    @pl.loop(1, npr)
    def _(p):
        project(p, False)

        @pl.loop(jnp.maximum(p - 2, 0) * cpp, (p - 1) * cpp)
        def _(t):
            chain(t)

    late(npr - 1)
    for p in range(npr):
        mine_out[p] = jnp.broadcast_to((own_ref[p] == me).astype(F32), mine_out.shape[1:])

    def inner(p):
        causal = iota((span, span), 0) >= iota((span, span), 1)
        keep = jnp.where(causal, live_row(p), 0.0)
        ones = jnp.ones((span, head_dim), BF)
        lane = iota((1, LANES), 1) // FD
        q, k = qs[p], ks[p].astype(F32)
        kt[0] = q.astype(F32).T
        for h in range(heads):
            mask = (lane == spot // FD + head_of(h)).astype(F32)
            s = dot(q, (k * mask).astype(BF), NT)
            w = ((1.0 + s * (FD ** -0.5 + s * (0.5 / FD))) * keep).astype(BF)
            vv = jnp.concatenate([vs[p, :, h * head_dim:(h + 1) * head_dim], ones], axis=1)
            nd[p, h] = dot(w, vv)
            phs[p, h] = features(kt[0, head_rows(h)], rows, weights).astype(BF).T

    sqsend[...] = jnp.zeros_like(sqsend)

    def flat(block):
        return block.reshape(half * rows, head_dim)

    def zrow_of(state):
        block = state[LIN:ONE + 8].astype(F32)
        return jnp.concatenate([block[ONE + 1 - LIN:ONE + 2 - LIN], block[ONE + 2 - LIN:ONE + 3 - LIN, :ONE + 8 - LANES]], axis=1)

    def outer(p):
        @pl.loop(0, cpp)
        def _(j):
            to_seq(fwd.at[p, j], pre.at[p, 0, j], s3, r3.at[p, j], mate).wait_recv()
        live = (iota((span, 1), 0) + me * span < len_ref[p]).astype(F32)
        earlier = jnp.minimum(me * span, len_ref[p]).astype(F32)
        sq = jnp.zeros((sqsend.shape[0], span), F32)
        for h in range(heads):
            state = flat(pre[p, h // half])[(h % half) * rows:(h % half + 1) * rows]
            zr = zrow_of(state)
            zr = jnp.where(iota(zr.shape, 1) == ONE, 0.0, zr)
            zb = jnp.broadcast_to(zr, (head_dim, zr.shape[1])).astype(BF)
            phit = phs[p, h]
            num = dot(phit, state) + nd[p, h, :, :head_dim]
            den = dot(phit[:, :zr.shape[1]], zb, NT) + nd[p, h, :, head_dim:] + earlier
            att = num / den * live
            att_out[p, :, pl.ds(pl.multiple_of(head_of(h) * head_dim, LANES), head_dim)] = att
            sq = sq + dot(jnp.ones((sqsend.shape[0], head_dim), BF), (att * att).astype(BF), NT)
        sqsend[...] = jnp.where(iota(sq.shape, 0) == p, sq, sqsend[...])

        @pl.when(p == npr - 1)
        def _():
            sqgot[fi] = sqsend[...]
            for i in range(1, nf):
                to_feat(sqsend, sqgot.at[fi], s4.at[i], r4.at[fi], lax.rem(fi + i, nf)).start()

    per = FD * FD // nf

    def spread(p, slot, total):
        c = 1 - yi if slot == 0 else yi
        pick = pick_matrix(0, FD * FD, rows).astype(BF)
        for i in range(half):
            h = c * half + i
            mine = total[i * rows:(i + 1) * rows].astype(BF)
            zr = zrow_of(mine)
            zr = jnp.where(iota(zr.shape, 1) == ONE, len_ref[p].astype(F32), zr)
            ztsend[pl.ds(p * heads + h, 1)] = zr
            full = dot(pick, mine).astype(BF)
            for f in range(nf):
                tsend[f, p, h] = full[f * per:(f + 1) * per]
            end = mine[LIN:].astype(F32)
            low_out[p, h] = jnp.concatenate(
                [end[ONE - LIN:ONE - LIN + 1], end[:FD] * FD ** -0.25], axis=0)
        for i in range(1, nf):
            spread_copy(p, c, i).start()
        which = pl.ds(c * half, half)
        quad_out[fi, p, which] = tsend[fi, p, which]

    def spread_copy(p, c, i):
        target = lax.rem(fi + i, nf)
        which = pl.ds(c * half, half)
        return to_feat(tsend.at[target, p, which], quad_out.at[fi, p, which], s5.at[i], r5.at[fi], target)

    def spread_own(p):
        spread(p, 1, flat(up_got[p].astype(F32) + bsum[p].astype(F32) + dn_got[p].astype(F32)))

    def spread_other(p):
        @pl.loop(0, cpp)
        def _(j):
            suf_copy(p, j).wait_recv()
        spread(p, 0, flat(pre[p, 0].astype(F32) + part[p, 0].astype(F32) + suf[p].astype(F32)))

    far = lag * jnp.maximum(zo, last - zo)

    early = (npr - 2) * cpp

    def step(t, _):
        chain(t)
        at((t - early) * 2, inner, cpp)
        done = t - cpp + 1 - turn
        at(done + turn - far, spread_own, cpp)
        at(done - jnp.where(below, lag * last, early), outer, cpp)
        at(done - lag * last, spread_other, cpp)
        return 0

    lax.fori_loop(early, chunks + lag * last + turn, step, 0)

    ztgot[fi] = ztsend[...]
    for i in range(1, nf):
        to_feat(ztsend, ztgot.at[fi], s6.at[i], r6.at[fi], lax.rem(fi + i, nf)).start()

    for i in range(1, nf):
        src = lax.rem(fi + i, nf)
        to_feat(sqsend, sqgot.at[src], s4.at[i], r4.at[src], fpeer).wait_recv()
        to_feat(tsend.at[src], quad_out.at[src], s5.at[i], r5.at[src], fpeer).wait_recv()
        to_feat(ztsend, ztgot.at[src], s6.at[i], r6.at[src], fpeer).wait_recv()
    for i in range(1, nf):
        to_feat(sqsend, sqgot.at[fi], s4.at[i], r4.at[fi], fpeer).wait_send()
        to_feat(tsend.at[fi], quad_out.at[fi], s5.at[i], r5.at[fi], fpeer).wait_send()
        to_feat(ztsend, ztgot.at[fi], s6.at[i], r6.at[fi], fpeer).wait_send()
    to_seq(fwd, fwd, s0, s0, mate).wait_send()
    to_seq(fwd, fwd, s3, s3, mate).wait_send()
    to_seq(bwd, bwd, s7, s7, mate).wait_send()

    @pl.when(above)
    def _():
        to_seq(up_send, up_send, s1, s1, mate).wait_send()

    @pl.when(below)
    def _():
        to_seq(dn_send, dn_send, s2, s2, mate).wait_send()


def finish(cfg, att, sq, quad, low, zt, mine, mixed_out, quad_out, low_out, nq_out, nl_out,
           mixed_buf, quad_buf, sem):
    nf, heads, npr, per = cfg
    span, width = att.shape[1], att.shape[2]
    fi = lax.axis_index("feat")
    squares = sq[0]
    for f in range(1, nf):
        squares = squares + sq[f]
    inv = lax.rsqrt(squares * (1.0 / (nf * width)) + NORM_FLOOR)
    writes = []
    for p in range(npr):
        mask = mine[p, :1]
        for f in range(nf):
            quad_buf[p, f * heads:(f + 1) * heads] = quad[f, p].astype(F32) * (mask * (2.0 * FD) ** -0.5)
        writes.append(pltpu.make_async_copy(quad_buf.at[p], quad_out.at[p], sem.at[0, p]))
        writes[-1].start()
        col = jnp.broadcast_to(inv[p:p + 1], (LANES, span)).T
        for c in range(width // LANES):
            mixed_buf[p, :, c * LANES:(c + 1) * LANES] = (att[p, :, c * LANES:(c + 1) * LANES] * col).astype(BF)
        writes.append(pltpu.make_async_copy(mixed_buf.at[p], mixed_out.at[p], sem.at[1, p]))
        writes[-1].start()
    own_pick = pick_matrix(fi * per, per, ONE + 8).astype(F32)
    lr, lc = iota((FD + 1, ONE + 8), 0), iota((FD + 1, ONE + 8), 1)
    low_pick = jnp.where(lr == 0, (lc == ONE).astype(F32), (lc == LIN - 1 + lr).astype(F32) * FD ** -0.25)
    nl = dot(zt[fi], low_pick, NT, lax.Precision.HIGHEST)
    for f in range(nf):
        nq = dot(zt[f], own_pick, NT, lax.Precision.HIGHEST) * (2.0 * FD) ** -0.5
        for p in range(npr):
            nq_out[p, f * heads:(f + 1) * heads] = nq[p * heads:(p + 1) * heads] * mine[p, :1, :per]
    for p in range(npr):
        nl_out[p] = nl[p * heads:(p + 1) * heads] * mine[p, :1, :FD + 1]
        for h in range(heads):
            low_out[p, :, h, :] = low[p, h] * mine[p, :1]
    for write in writes:
        write.wait()


def body(hidden_in, w_query, w_key, w_value, lengths, owners):
    npr, span, width = hidden_in.shape
    n, nf = lax.axis_size("seq"), lax.axis_size("feat")
    heads = H // nf
    head_dim = width // H
    rows = -(-LIVE_ROWS // 16) * 16
    half_rows = heads // 2 * rows
    cpp, lag, turn = 2, 3, 3
    cfg = (n, nf, npr, span, heads, rows, cpp, lag, turn)
    per = FD * FD // nf
    chunk = (cpp, half_rows // cpp, head_dim)
    dma = pltpu.SemaphoreType.DMA
    vm = pltpu.VMEM
    ph = npr * heads
    out = pl.pallas_call(
        functools.partial(kernel, cfg),
        out_shape=(
            vm((npr, span, heads * head_dim), F32),
            vm((nf, 8, span), F32),
            vm((nf, npr, heads, per, head_dim), BF),
            vm((npr, heads, FD + 1, head_dim), F32),
            vm((nf, ph, ONE + 8), F32),
            vm((npr, 8, LANES), F32),
        ),
        in_specs=[pl.BlockSpec(memory_space=pltpu.HBM)] * 6,
        out_specs=[pl.BlockSpec(memory_space=pltpu.VMEM)] * 6,
        scratch_shapes=[
            vm((npr, span, width), BF),
            vm((width, 2 * LANES + heads * head_dim), BF),
            vm((npr, span, LANES), BF),
            vm((npr, span, LANES), BF),
            vm((npr, span, heads * head_dim), BF),
            vm((2, LANES, span), F32),
            vm((npr, heads, span, rows), BF),
            vm((npr, heads, span, 2 * head_dim), F32),
            vm((npr, 2) + chunk, BF),
            *[vm((npr,) + chunk, BF)] * 7,
            vm((npr, 2) + chunk, BF),
            *[vm((npr,) + chunk, BF)] * 2,
            vm((nf, npr, heads, per, head_dim), BF),
            vm((8, span), F32),
            vm((ph, ONE + 8), F32),
            pltpu.SMEM((npr,), jnp.int32),
            pltpu.SMEM((npr,), jnp.int32),
            dma((npr + 6,)),
            *[dma, dma((npr, cpp))] * 4,
            *[dma((nf,))] * 6,
            dma, dma((npr, cpp)),
        ],
        compiler_params=pltpu.CompilerParams(
            collective_id=0, has_side_effects=True, vmem_limit_bytes=40 * 1024 * 1024
        ),
        name="layer",
    )(*[pltpu.with_memory_space_constraint(a, pltpu.HBM) for a in (lengths, owners, hidden_in, w_query, w_key, w_value)])
    onchip = [pltpu.with_memory_space_constraint(o, pltpu.VMEM) for o in out]
    block = pl.BlockSpec
    mixed, quad, low, nq, nl = pl.pallas_call(
        functools.partial(finish, (nf, heads, npr, per)),
        out_shape=(
            jax.ShapeDtypeStruct((npr, span, heads * head_dim), BF),
            jax.ShapeDtypeStruct((npr, H, per, head_dim), F32),
            jax.ShapeDtypeStruct((npr, FD + 1, heads, head_dim), F32),
            jax.ShapeDtypeStruct((npr, H, per), F32),
            jax.ShapeDtypeStruct((npr, heads, FD + 1), F32),
        ),
        in_specs=[block(memory_space=pltpu.VMEM)] * 6,
        out_specs=[block(memory_space=pl.ANY)] * 2 + [block(memory_space=pltpu.VMEM)] * 3,
        scratch_shapes=[
            vm((npr, span, heads * head_dim), BF),
            vm((npr, H, per, head_dim), F32),
            dma((2, npr)),
        ],
        compiler_params=pltpu.CompilerParams(vmem_limit_bytes=16 * 1024 * 1024),
        name="finish",
    )(*onchip)
    return (mixed, quad[None], jnp.transpose(low, (0, 2, 1, 3))[None], nq[None], nl[None])


def solution(mesh):
    placed = (P(None, "seq", None), P(), P(), P(None, "feat"), P(), P())
    return jax.shard_map(
        body,
        mesh=mesh,
        in_specs=placed,
        out_specs=(
            P(None, "seq", "feat"),
            P("seq", None, None, "feat", None),
            P("seq", None, "feat", None, None),
            P("seq", None, None, "feat"),
            P("seq", None, "feat", None),
        ),
        check_vma=False,
    )
```

time: 48.3 us -> 39.3 us (0.81)
  Pallas kernels: 46.8 us -> 38.5 us
  local copies, waits for them, and re-layouts: 0.65 us -> 0 us
    pallas_call x1, Pallas kernels: 43.6 us -> 35.8 us  [body(): pl.pallas_call(functools.partial(kernel, cfg), out_shape=(vm((npr, span,...]
    unnamed x4 -> x0, local copies, waits for them, and re-layouts: 0.65 us -> none
    pallas_call x1, Pallas kernels: 3.24 us -> 2.73 us  [body(): pl.pallas_call(functools.partial(finish, (nf, heads, npr, per)), out_shap...]
where the time goes in v2:
time: 39.3 us; the launch traced here: 39.2 us
  Pallas kernels  38.5 us (98%)
  between operations  0.64 us (2%)
    pallas_call x1, Pallas kernels, body(): pl.pallas_call(functools.partial(kernel, cfg), out_shape=(vm((npr, span,...  35.8 us
    pallas_call x1, Pallas kernels, body(): pl.pallas_call(functools.partial(finish, (nf, heads, npr, per)), out_shap...  2.73 us

profile of v2, /device:TPU:0, one launch (start us, length us, event | category | flops | bytes accessed | tf_op | source)
XLA Modules:
  0.0 39.2 jit_solution(15589154179345431907)
XLA Ops:
  0.6 35.8 %layer.1 = (f32[4,256,512]{2,1,0:T(8,128)S(1)}, f32[4,8,256]{2,1,0:T(8,128)S(1)}, bf16[4,4,4,64,128]{4,3,2,1,0:T(8,128)(2,1)S(1)}, f32[4,4,17,128]{3,2,1,0:T(8,1...) custom-call(s32[4]{0:T(128)} %len_hbm.1, s32[4]{0:T(128)} %own_hbm.1, bf16[4,256,2048]{2,1,0:T(8,128)(2,1)} %x_hbm.1, ...), custom_call_target="tpu_custom_call" | custom-call | tf_op jit(solution)/shard_map/layer/pallas_call | solution.py:458
  36.4 2.7 %finish.1 = (bf16[4,256,512]{2,1,0:T(8,128)(2,1)}, f32[4,16,64,128]{3,2,1,0:T(8,128)}, f32[4,17,4,128]{3,2,1,0:T(4,128)}, f32[4,16,64]{2,1,0:T(8,128)}, f32[4,4,17]{2,1,0:T(4,128)}) custom-call(f32[4,256,512]{2,1,0:T(8,128)S(1)} %get-tuple-element.16.att, f32[4,8,256]{2,1,0:T(8,128)S(1)} %get-tuple-element.17.sq, ...), custom_call_target="tpu_custom_call" | custom-call | tf_op jit(solution)/shard_map/finish/pallas_call | solution.py:500

commit v3 on v2

--- a/solution.py
+++ b/solution.py
@@ -56,11 +56,12 @@
 
 
 def kernel(cfg, len_hbm, own_hbm, x_hbm, wq_hbm, wk_hbm, wv_hbm,
-           att_out, sqgot, quad_out, low_out, ztgot, mine_out,
+           att_out, sqgot, quad_out, low_out, mine_out,
            hid, wall, qs, ks, vs, kt, phs, nd, part, mgot, bsum, up_got, up_send, dn_got, dn_send,
-           fwd, pre, bwd, suf, tsend, sqsend, ztsend, len_ref, own_ref,
-           in_sem, s0, r0, s1, r1, s2, r2, s3, r3, s4, r4, s5, r5, s6, r6, s7, r7):
-    n, nf, npr, span, heads, rows, cpp, lag, turn = cfg
+           fwd, pre, bwd, suf, tsend, sqsend, pick, len_ref, own_ref,
+           in_sem, s0, r0, s1, r1, s2, r2, s3, r3, s4, r4, s5, r5, s8, s9, s12, r12, s7, r7):
+    n, nf, npr, span, heads, rows, cpp, lag, turn, direct = cfg
+    relayed = npr - direct
     me, fi = lax.axis_index("seq"), lax.axis_index("feat")
     own = heads * FD
     half = heads // 2
@@ -77,47 +78,58 @@
         return pl.ds(pl.multiple_of(c * hw, LANES), hw)
 
     base = pl.multiple_of((fi * own // LANES) * LANES, LANES)
-    qk_loads = [
-        pltpu.make_async_copy(wq_hbm.at[:, pl.ds(base, LANES)], wall.at[:, pl.ds(0, LANES)], in_sem.at[npr]),
-        pltpu.make_async_copy(wk_hbm.at[:, pl.ds(base, LANES)], wall.at[:, pl.ds(LANES, LANES)], in_sem.at[npr + 1]),
+    middle = wall.shape[0] // 2
+    parts = (pl.ds(0, middle), pl.ds(middle, middle))
+
+    def first_loads(i):
+        r, sems = parts[i], in_sem.at[npr + i]
+        mate_cols = half_cols(1 - yi)
+        return [
+            pltpu.make_async_copy(x_hbm.at[0, :, r], hid.at[0, :, r], sems.at[0]),
+            pltpu.make_async_copy(wq_hbm.at[r, pl.ds(base, LANES)], wall.at[r, pl.ds(0, LANES)], sems.at[1]),
+            pltpu.make_async_copy(wk_hbm.at[r, pl.ds(base, LANES)], wall.at[r, pl.ds(LANES, LANES)], sems.at[2]),
+            pltpu.make_async_copy(wv_hbm.at[r, mate_cols], wall.at[r, pl.ds(2 * LANES, hw)], sems.at[3]),
+        ]
+
+    own_load = pltpu.make_async_copy(wv_hbm.at[:, half_cols(yi)], wall.at[:, pl.ds(2 * LANES + hw, hw)], in_sem.at[0, 0])
+    small = [
+        pltpu.make_async_copy(len_hbm, len_ref, in_sem.at[0, 1]),
+        pltpu.make_async_copy(own_hbm, own_ref, in_sem.at[0, 2]),
     ]
 
-    def v_load(step):
-        cols = half_cols(1 - yi if step == 0 else yi)
-        return pltpu.make_async_copy(wv_hbm.at[:, cols], wall.at[:, pl.ds(2 * LANES + step * hw, hw)], in_sem.at[npr + 2 + step])
-
     def hid_copy(p):
-        return pltpu.make_async_copy(x_hbm.at[p], hid.at[p], in_sem.at[p])
-
-    for load in qk_loads:
-        load.start()
-    hid_copy(0).start()
-    v_load(0).start()
-    v_load(1).start()
-    small = [
-        pltpu.make_async_copy(len_hbm, len_ref, in_sem.at[npr + 4]),
-        pltpu.make_async_copy(own_hbm, own_ref, in_sem.at[npr + 5]),
-    ]
+        return pltpu.make_async_copy(x_hbm.at[p], hid.at[p], in_sem.at[p, 3])
+
+    for i in range(2):
+        for load in first_loads(i):
+            load.start()
     for load in small:
         load.start()
+    own_load.start()
 
     barrier = pltpu.get_barrier_semaphore()
 
-    def greet(axis, target):
-        pl.semaphore_signal(barrier, 1, device_id={axis: target}, device_id_type=pl.DeviceIdType.MESH)
-
-    greet("seq", mate)
+    def greet(**target):
+        pl.semaphore_signal(barrier, 1, device_id=target, device_id_type=pl.DeviceIdType.MESH)
+
+    greet(seq=mate)
 
     @pl.when(below)
     def _():
-        greet("seq", me - 2)
+        greet(seq=me - 2)
 
     @pl.when(above)
     def _():
-        greet("seq", me + 2)
+        greet(seq=me + 2)
 
     for i in range(1, nf):
-        greet("feat", lax.rem(fi + i, nf))
+        greet(feat=lax.rem(fi + i, nf))
+        greet(seq=mate, feat=lax.rem(fi + i, nf))
+
+    sqsend[...] = jnp.zeros_like(sqsend)
+    pick[...] = pick_matrix(0, FD * FD, rows).astype(BF)
+    send_pre, take_pre = below | (yi == 0), below | (yi == 1)
+    send_suf, take_suf = above | (yi == 1), above | (yi == 0)
 
     @pl.when(zo == 0)
     def _():
@@ -126,6 +138,14 @@
     @pl.when(zo == last)
     def _():
         dn_got[...] = jnp.zeros(dn_got.shape, BF)
+
+    @pl.when(jnp.logical_not(take_pre))
+    def _():
+        pre[:, 0] = jnp.zeros((npr,) + pre.shape[2:], BF)
+
+    @pl.when(jnp.logical_not(take_suf))
+    def _():
+        suf[...] = jnp.zeros(suf.shape, BF)
 
     def to_seq(src, dst, ssem, rsem, target):
         return pltpu.make_async_remote_copy(
@@ -136,6 +156,11 @@
         return pltpu.make_async_remote_copy(
             src_ref=src, dst_ref=dst, send_sem=ssem, recv_sem=rsem,
             device_id={"feat": target}, device_id_type=pl.DeviceIdType.MESH)
+
+    def to_mates(src, dst, ssem, rsem, target):
+        return pltpu.make_async_remote_copy(
+            src_ref=src, dst_ref=dst, send_sem=ssem, recv_sem=rsem,
+            device_id={"seq": mate, "feat": target}, device_id_type=pl.DeviceIdType.MESH)
 
     fpeer = lax.rem(fi + 1, nf)
 
@@ -180,21 +205,20 @@
     def head_rows(slot):
         return pl.ds(pl.multiple_of(spot + head_of(slot) * FD, FD), FD)
 
-    for load in qk_loads:
-        load.wait()
-    v_load(0).wait()
-    for load in small:
-        load.wait()
-    hid_copy(0).wait()
-    for p in range(1, npr):
-        hid_copy(p).start()
-    middle = wall.shape[0] // 2
-
     def project(p, first):
-        if not first:
+        cols = slice(0, 2 * LANES + hw)
+        if first:
+            for load in first_loads(0):
+                load.wait()
+            head = dot(hid[p, :, :middle], wall[:middle, cols])
+            for load in first_loads(1):
+                load.wait()
+            for later in range(1, npr):
+                hid_copy(later).start()
+            head = head + dot(hid[p, :, middle:], wall[middle:, cols])
+        else:
             hid_copy(p).wait()
-        x = hid[p]
-        head = dot(x, wall[:, :2 * LANES + hw])
+            head = dot(hid[p], wall[:, cols])
         k = head[:, LANES:2 * LANES].astype(BF)
         qs[p] = head[:, :LANES].astype(BF)
         ks[p] = k
@@ -203,14 +227,17 @@
         v = head[:, 2 * LANES:].astype(BF)
         vs[p, :, :hw] = v
         if first:
-            v_load(1).wait()
+            own_load.wait()
+            for load in small:
+                load.wait()
         else:
             late(p - 1)
-        mine = dot(x[:, :middle], wall[:middle, 2 * LANES + hw:]) + dot(x[:, middle:], wall[middle:, 2 * LANES + hw:])
+        mine = jnp.concatenate(
+            [dot(hid[p, r * span // 2:(r + 1) * span // 2], wall[:, 2 * LANES + hw:]) for r in range(2)], axis=0)
         part[p, 0] = sums_of(0, slot, v, live_row(p))
         vs[p, :, hw:] = mine.astype(BF)
         if first:
-            pl.semaphore_wait(barrier, nf + below.astype(jnp.int32) + above.astype(jnp.int32))
+            pl.semaphore_wait(barrier, 2 * nf - 1 + below.astype(jnp.int32) + above.astype(jnp.int32))
         for j in range(cpp):
             swap_copy(p, j).start()
 
@@ -235,7 +262,10 @@
             up_send[p, j] = (up_got[p, j].astype(F32) + bsum[p, j].astype(F32)).astype(BF)
             up_copy(p, j).start()
         fwd[p, j] = (before + jnp.where(yi == 0, part[p, 1, j].astype(F32), 0.0)).astype(BF)
-        pre_copy(p, j).start()
+
+        @pl.when(below)
+        def _():
+            pre_copy(p, j).start()
         pre[p, 1, j] = (before + jnp.where(yi == 1, mgot[p, j].astype(F32), 0.0)).astype(BF)
 
     def take_down(k):
@@ -251,7 +281,10 @@
             dn_send[p, j] = (dn_got[p, j].astype(F32) + bsum[p, j].astype(F32)).astype(BF)
             dn_copy(p, j).start()
         bwd[p, j] = (after + jnp.where(yi == 1, part[p, 1, j].astype(F32), 0.0)).astype(BF)
-        suf_copy(p, j).start()
+
+        @pl.when(above & (p < relayed))
+        def _():
+            suf_copy(p, j).start()
 
     def at(t, body, stride=1):
         @pl.when((t >= 0) & (t < chunks) & (lax.rem(t, stride) == 0))
@@ -275,7 +308,7 @@
 
     late(npr - 1)
     for p in range(npr):
-        mine_out[p] = jnp.broadcast_to((own_ref[p] == me).astype(F32), mine_out.shape[1:])
+        mine_out[p] = jnp.where(iota(mine_out.shape[1:], 0) == 1, len_ref[p].astype(F32), (own_ref[p] == me).astype(F32))
 
     def inner(p):
         causal = iota((span, span), 0) >= iota((span, span), 1)
@@ -292,7 +325,6 @@
             nd[p, h] = dot(w, vv)
             phs[p, h] = features(kt[0, head_rows(h)], rows, weights).astype(BF).T
 
-    sqsend[...] = jnp.zeros_like(sqsend)
 
     def flat(block):
         return block.reshape(half * rows, head_dim)
@@ -301,25 +333,35 @@
         block = state[LIN:ONE + 8].astype(F32)
         return jnp.concatenate([block[ONE + 1 - LIN:ONE + 2 - LIN], block[ONE + 2 - LIN:ONE + 3 - LIN, :ONE + 8 - LANES]], axis=1)
 
-    def outer(p):
-        @pl.loop(0, cpp)
-        def _(j):
-            to_seq(fwd.at[p, j], pre.at[p, 0, j], s3, r3.at[p, j], mate).wait_recv()
+    def outer(p, mates):
         live = (iota((span, 1), 0) + me * span < len_ref[p]).astype(F32)
         earlier = jnp.minimum(me * span, len_ref[p]).astype(F32)
-        sq = jnp.zeros((sqsend.shape[0], span), F32)
-        for h in range(heads):
-            state = flat(pre[p, h // half])[(h % half) * rows:(h % half + 1) * rows]
+        squares = jnp.zeros((span, head_dim), F32)
+        for i in range(half):
+            slot = i if mates else half + i
+            head = (1 - yi if mates else yi) * half + i
+            state = pre[p, 0 if mates else 1, i]
             zr = zrow_of(state)
             zr = jnp.where(iota(zr.shape, 1) == ONE, 0.0, zr)
             zb = jnp.broadcast_to(zr, (head_dim, zr.shape[1])).astype(BF)
-            phit = phs[p, h]
-            num = dot(phit, state) + nd[p, h, :, :head_dim]
-            den = dot(phit[:, :zr.shape[1]], zb, NT) + nd[p, h, :, head_dim:] + earlier
+            phit = phs[p, slot]
+            num = dot(phit, state) + nd[p, slot, :, :head_dim]
+            den = dot(phit[:, :zr.shape[1]], zb, NT) + nd[p, slot, :, head_dim:] + earlier
             att = num / den * live
-            att_out[p, :, pl.ds(pl.multiple_of(head_of(h) * head_dim, LANES), head_dim)] = att
-            sq = sq + dot(jnp.ones((sqsend.shape[0], head_dim), BF), (att * att).astype(BF), NT)
-        sqsend[...] = jnp.where(iota(sq.shape, 0) == p, sq, sqsend[...])
+            att_out[p, :, pl.ds(pl.multiple_of(head * head_dim, LANES), head_dim)] = att
+            squares = squares + att * att
+        sq = dot(jnp.ones((sqsend.shape[0], head_dim), BF), squares.astype(BF), NT)
+        sqsend[...] += jnp.where(iota(sq.shape, 0) == p, sq, 0.0)
+
+    def outer_own(p):
+        outer(p, False)
+
+    def outer_other(p):
+        @pl.when(take_pre)
+        def _():
+            for j in range(cpp):
+                pre_copy(p, j).wait_recv()
+        outer(p, True)
 
         @pl.when(p == npr - 1)
         def _():
@@ -329,71 +371,96 @@
 
     per = FD * FD // nf
 
-    def spread(p, slot, total):
-        c = 1 - yi if slot == 0 else yi
-        pick = pick_matrix(0, FD * FD, rows).astype(BF)
+    def spread(p, c, totals):
+        mine = [total.astype(BF) for total in totals]
+        full = dot(pick[...], jnp.concatenate(mine, axis=1)).astype(BF)
+        zrows = [zrow_of(m) for m in mine]
+        fill = jnp.zeros((8 - half, zrows[0].shape[1]), F32)
+        zq = dot(jnp.concatenate(zrows + [fill], axis=0).astype(BF), pick[...], NT)
+        blank = jnp.zeros((8, head_dim - per), F32)
+        for f in range(nf):
+            for i in range(half):
+                tsend[f, p, c, i * per:(i + 1) * per] = full[f * per:(f + 1) * per, i * head_dim:(i + 1) * head_dim]
+            tsend[f, p, c, half * per:] = jnp.concatenate([zq[:, f * per:(f + 1) * per], blank], axis=1).astype(BF)
+        last_one = p >= relayed
+
+        @pl.when(jnp.logical_not(last_one))
+        def _():
+            for i in range(1, nf):
+                target = lax.rem(fi + i, nf)
+                to_feat(tsend.at[target, p, c], quad_out.at[fi, p, c], s5.at[i], r5.at[fi], target).start()
+        quad_out[fi, p, c] = tsend[fi, p, c]
         for i in range(half):
-            h = c * half + i
-            mine = total[i * rows:(i + 1) * rows].astype(BF)
-            zr = zrow_of(mine)
-            zr = jnp.where(iota(zr.shape, 1) == ONE, len_ref[p].astype(F32), zr)
-            ztsend[pl.ds(p * heads + h, 1)] = zr
-            full = dot(pick, mine).astype(BF)
-            for f in range(nf):
-                tsend[f, p, h] = full[f * per:(f + 1) * per]
-            end = mine[LIN:].astype(F32)
-            low_out[p, h] = jnp.concatenate(
-                [end[ONE - LIN:ONE - LIN + 1], end[:FD] * FD ** -0.25], axis=0)
-        for i in range(1, nf):
-            spread_copy(p, c, i).start()
+            end = mine[i][LIN:].astype(F32)
+            lows = end[:FD] * FD ** -0.25
+            count = jnp.where(iota((1, 1), 0) == 0, len_ref[p].astype(F32), 0.0)
+            zlow = jnp.concatenate([count, end[ONE + 2 - LIN:ONE + 3 - LIN, :FD] * FD ** -0.25, jnp.zeros((1, head_dim - FD - 1), F32)], axis=1)
+            low_out[p, c * half + i] = jnp.concatenate(
+                [end[ONE - LIN:ONE - LIN + 1], lows, zlow, jnp.zeros((6, head_dim), F32)], axis=0)
+
+
+    def low_copy(p, c):
         which = pl.ds(c * half, half)
-        quad_out[fi, p, which] = tsend[fi, p, which]
-
-    def spread_copy(p, c, i):
-        target = lax.rem(fi + i, nf)
-        which = pl.ds(c * half, half)
-        return to_feat(tsend.at[target, p, which], quad_out.at[fi, p, which], s5.at[i], r5.at[fi], target)
+        return to_seq(low_out.at[p, which], low_out.at[p, which], s12, r12, mate)
 
     def spread_own(p):
-        spread(p, 1, flat(up_got[p].astype(F32) + bsum[p].astype(F32) + dn_got[p].astype(F32)))
+        spread(p, yi, [up_got[p, j].astype(F32) + bsum[p, j].astype(F32) + dn_got[p, j].astype(F32) for j in range(cpp)])
 
     def spread_other(p):
-        @pl.loop(0, cpp)
-        def _(j):
-            suf_copy(p, j).wait_recv()
-        spread(p, 0, flat(pre[p, 0].astype(F32) + part[p, 0].astype(F32) + suf[p].astype(F32)))
-
-    far = lag * jnp.maximum(zo, last - zo)
+        @pl.when(take_suf)
+        def _():
+            for j in range(cpp):
+                suf_copy(p, j).wait_recv()
+        spread(p, 1 - yi, [pre[p, 0, j].astype(F32) + part[p, 0, j].astype(F32) + suf[p, j].astype(F32) for j in range(cpp)])
+
+    def held_pre(k):
+        pre_copy(k // cpp, lax.rem(k, cpp)).start()
+
+    def held_suf(k):
+        @pl.when(k < relayed * cpp)
+        def _():
+            suf_copy(k // cpp, lax.rem(k, cpp)).start()
 
     early = (npr - 2) * cpp
+    reach = max(lag * last, early + npr)
+    far = jnp.maximum(lag * jnp.maximum(zo, last - zo), early)
+
+    hold = early
 
     def step(t, _):
         chain(t)
+        at(t - jnp.where(jnp.logical_not(below) & send_pre, hold, chunks + t), held_pre)
+        at(t - jnp.where(jnp.logical_not(above) & send_suf, hold, chunks + t), held_suf)
         at((t - early) * 2, inner, cpp)
-        done = t - cpp + 1 - turn
-        at(done + turn - far, spread_own, cpp)
-        at(done - jnp.where(below, lag * last, early), outer, cpp)
-        at(done - lag * last, spread_other, cpp)
+        base_own = jnp.where(below, reach, early + npr)
+        back = t - cpp + 1
+        at(back - base_own - turn, outer_other, cpp)
+        at(back - far, spread_own, cpp)
+        at(back - base_own, outer_own, cpp)
+        mine = back - reach - turn
+        at(jnp.where(mine < relayed * cpp, mine, -1), spread_other, cpp)
         return 0
 
-    lax.fori_loop(early, chunks + lag * last + turn, step, 0)
-
-    ztgot[fi] = ztsend[...]
-    for i in range(1, nf):
-        to_feat(ztsend, ztgot.at[fi], s6.at[i], r6.at[fi], lax.rem(fi + i, nf)).start()
-
+    lax.fori_loop(early, chunks + reach + turn, step, 0)
+
+    ends, starts = pl.ds(relayed, direct), pl.ds(0, relayed)
+    own_side, mate_side = pl.ds(yi * half, half), pl.ds((1 - yi) * half, half)
     for i in range(1, nf):
         src = lax.rem(fi + i, nf)
         to_feat(sqsend, sqgot.at[src], s4.at[i], r4.at[src], fpeer).wait_recv()
         to_feat(tsend.at[src], quad_out.at[src], s5.at[i], r5.at[src], fpeer).wait_recv()
-        to_feat(ztsend, ztgot.at[src], s6.at[i], r6.at[src], fpeer).wait_recv()
     for i in range(1, nf):
         to_feat(sqsend, sqgot.at[fi], s4.at[i], r4.at[fi], fpeer).wait_send()
-        to_feat(tsend.at[fi], quad_out.at[fi], s5.at[i], r5.at[fi], fpeer).wait_send()
-        to_feat(ztsend, ztgot.at[fi], s6.at[i], r6.at[fi], fpeer).wait_send()
+        to_feat(tsend.at[fi, starts], quad_out.at[fi, starts], s5.at[i], r5.at[fi], fpeer).wait_send()
     to_seq(fwd, fwd, s0, s0, mate).wait_send()
-    to_seq(fwd, fwd, s3, s3, mate).wait_send()
-    to_seq(bwd, bwd, s7, s7, mate).wait_send()
+
+    @pl.when(send_pre)
+    def _():
+        to_seq(fwd, fwd, s3, s3, mate).wait_send()
+
+    @pl.when(send_suf)
+    def _():
+        to_seq(bwd.at[starts], bwd.at[starts], s7, s7, mate).wait_send()
 
     @pl.when(above)
     def _():
@@ -404,20 +471,25 @@
         to_seq(dn_send, dn_send, s2, s2, mate).wait_send()
 
 
-def finish(cfg, att, sq, quad, low, zt, mine, mixed_out, quad_out, low_out, nq_out, nl_out,
+def finish(cfg, att, sq, quad, low, mine, mixed_out, quad_out, low_out, nq_out, nl_out,
            mixed_buf, quad_buf, sem):
     nf, heads, npr, per = cfg
     span, width = att.shape[1], att.shape[2]
-    fi = lax.axis_index("feat")
+    half = heads // 2
+    scale = (2.0 * FD) ** -0.5
     squares = sq[0]
     for f in range(1, nf):
         squares = squares + sq[f]
     inv = lax.rsqrt(squares * (1.0 / (nf * width)) + NORM_FLOOR)
     writes = []
     for p in range(npr):
-        mask = mine[p, :1]
+        mask = mine[p, :1] * scale
         for f in range(nf):
-            quad_buf[p, f * heads:(f + 1) * heads] = quad[f, p].astype(F32) * (mask * (2.0 * FD) ** -0.5)
+            for c in range(2):
+                block = quad[f, p, c].astype(F32) * mask
+                for i in range(half):
+                    quad_buf[p, f * heads + c * half + i] = block[i * per:(i + 1) * per]
+                nq_out[p, f * heads + c * half:f * heads + (c + 1) * half] = block[half * per:half * per + half, :per]
         writes.append(pltpu.make_async_copy(quad_buf.at[p], quad_out.at[p], sem.at[0, p]))
         writes[-1].start()
         col = jnp.broadcast_to(inv[p:p + 1], (LANES, span)).T
@@ -425,18 +497,11 @@
             mixed_buf[p, :, c * LANES:(c + 1) * LANES] = (att[p, :, c * LANES:(c + 1) * LANES] * col).astype(BF)
         writes.append(pltpu.make_async_copy(mixed_buf.at[p], mixed_out.at[p], sem.at[1, p]))
         writes[-1].start()
-    own_pick = pick_matrix(fi * per, per, ONE + 8).astype(F32)
-    lr, lc = iota((FD + 1, ONE + 8), 0), iota((FD + 1, ONE + 8), 1)
-    low_pick = jnp.where(lr == 0, (lc == ONE).astype(F32), (lc == LIN - 1 + lr).astype(F32) * FD ** -0.25)
-    nl = dot(zt[fi], low_pick, NT, lax.Precision.HIGHEST)
-    for f in range(nf):
-        nq = dot(zt[f], own_pick, NT, lax.Precision.HIGHEST) * (2.0 * FD) ** -0.5
-        for p in range(npr):
-            nq_out[p, f * heads:(f + 1) * heads] = nq[p * heads:(p + 1) * heads] * mine[p, :1, :per]
     for p in range(npr):
-        nl_out[p] = nl[p * heads:(p + 1) * heads] * mine[p, :1, :FD + 1]
         for h in range(heads):
-            low_out[p, :, h, :] = low[p, h] * mine[p, :1]
+            full = low[p, h] * mine[p, :1]
+            low_out[p, :, h, :] = full[:FD + 1]
+            nl_out[p, h:h + 1] = full[FD + 1:FD + 2, :FD + 1]
     for write in writes:
         write.wait()
 
@@ -448,25 +513,23 @@
     head_dim = width // H
     rows = -(-LIVE_ROWS // 16) * 16
     half_rows = heads // 2 * rows
-    cpp, lag, turn = 2, 3, 3
-    cfg = (n, nf, npr, span, heads, rows, cpp, lag, turn)
+    cpp, lag, turn = heads // 2, 3, 3
+    cfg = (n, nf, npr, span, heads, rows, cpp, lag, turn, 0)
     per = FD * FD // nf
     chunk = (cpp, half_rows // cpp, head_dim)
     dma = pltpu.SemaphoreType.DMA
     vm = pltpu.VMEM
-    ph = npr * heads
     out = pl.pallas_call(
         functools.partial(kernel, cfg),
         out_shape=(
             vm((npr, span, heads * head_dim), F32),
             vm((nf, 8, span), F32),
-            vm((nf, npr, heads, per, head_dim), BF),
-            vm((npr, heads, FD + 1, head_dim), F32),
-            vm((nf, ph, ONE + 8), F32),
+            vm((nf, npr, 2, heads // 2 * per + 8, head_dim), BF),
+            vm((npr, heads, 24, head_dim), F32),
             vm((npr, 8, LANES), F32),
         ),
         in_specs=[pl.BlockSpec(memory_space=pltpu.HBM)] * 6,
-        out_specs=[pl.BlockSpec(memory_space=pltpu.VMEM)] * 6,
+        out_specs=[pl.BlockSpec(memory_space=pltpu.VMEM)] * 5,
         scratch_shapes=[
             vm((npr, span, width), BF),
             vm((width, 2 * LANES + heads * head_dim), BF),
@@ -480,14 +543,15 @@
             *[vm((npr,) + chunk, BF)] * 7,
             vm((npr, 2) + chunk, BF),
             *[vm((npr,) + chunk, BF)] * 2,
-            vm((nf, npr, heads, per, head_dim), BF),
+            vm((nf, npr, 2, heads // 2 * per + 8, head_dim), BF),
             vm((8, span), F32),
-            vm((ph, ONE + 8), F32),
+            vm((FD * FD, rows), BF),
             pltpu.SMEM((npr,), jnp.int32),
             pltpu.SMEM((npr,), jnp.int32),
-            dma((npr + 6,)),
+            dma((npr + 2, 4)),
             *[dma, dma((npr, cpp))] * 4,
             *[dma((nf,))] * 6,
+            dma, dma,
             dma, dma((npr, cpp)),
         ],
         compiler_params=pltpu.CompilerParams(
@@ -506,7 +570,7 @@
             jax.ShapeDtypeStruct((npr, H, per), F32),
             jax.ShapeDtypeStruct((npr, heads, FD + 1), F32),
         ),
-        in_specs=[block(memory_space=pltpu.VMEM)] * 6,
+        in_specs=[block(memory_space=pltpu.VMEM)] * 5,
         out_specs=[block(memory_space=pl.ANY)] * 2 + [block(memory_space=pltpu.VMEM)] * 3,
         scratch_shapes=[
             vm((npr, span, heads * head_dim), BF),

time: 39.3 us -> 38.3 us (0.975)
  Pallas kernels: 38.5 us -> 37.5 us
    pallas_call x1, Pallas kernels: 35.8 us -> 35 us  [body(): pl.pallas_call(functools.partial(kernel, cfg), out_shape=(vm((npr, span,...]
where the time goes in v3:
time: 38.3 us; the launch traced here: 38.2 us
  Pallas kernels  37.5 us (98%)
  between operations  0.64 us (2%)
    pallas_call x1, Pallas kernels, body(): pl.pallas_call(functools.partial(kernel, cfg), out_shape=(vm((npr, span,...  35 us
    pallas_call x1, Pallas kernels, body(): pl.pallas_call(functools.partial(finish, (nf, heads, npr, per)), out_shap...  2.52 us

profile of v3, /device:TPU:0, one launch (start us, length us, event | category | flops | bytes accessed | tf_op | source)
XLA Modules:
  0.0 38.2 jit_solution(15236083496456042230)
XLA Ops:
  0.6 35.0 %layer.1 = (f32[4,256,512]{2,1,0:T(8,128)S(1)}, f32[4,8,256]{2,1,0:T(8,128)S(1)}, bf16[4,4,2,136,128]{4,3,2,1,0:T(8,128)(2,1)S(1)}, f32[4,4,24,128]{3,2,1,0:T(8,128)S(1)}, f32[4,8,128]{2,1,0:T(8,128)S(1)}) custom-call(s32[4]{0:T(128)} %len_hbm.1, s32[4]{0:T(128)} %own_hbm.1, bf16[4,256,2048]{2,1,0:T(8,128)(2,1)} %x_hbm.1, bf16[2048,256]{1,0:T(8,128)(2,1)} %wq_hbm.1, ...), custom_call_target="tpu_custom_call" | custom-call | tf_op jit(solution)/shard_map/layer/pallas_call | solution.py:522
  35.7 2.5 %finish.1 = (bf16[4,256,512]{2,1,0:T(8,128)(2,1)}, f32[4,16,64,128]{3,2,1,0:T(8,128)}, f32[4,17,4,128]{3,2,1,0:T(4,128)}, f32[4,16,64]{2,1,0:T(8,128)}, f32[4,4,17]{2,1,0:T(4,128)}) custom-call(f32[4,256,512]{2,1,0:T(8,128)S(1)} %get-tuple-element.15.att, f32[4,8,256]{2,1,0:T(8,128)S(1)} %get-tuple-element.16.sq, ...), custom_call_target="tpu_custom_call" | custom-call | tf_op jit(solution)/shard_map/finish/pallas_call | solution.py:564
